TPU v7x, 256 devices: a whole 4x4x8 slice. The times are simulated.
256 devices in a mesh: row: 16 (over x, z_lo, core), col: 16 (over y, z_hi).
Axes of the slice: x: 4, y: 4, z: 8 (z_hi: 4, z_lo: 2; z = z_hi * 2 + z_lo), core: 2. Of those that a mesh axis runs over, the one named last changes fastest.
Arguments:
- dosage: bfloat16 [1536, 196608], P(None, ('row', 'col')), may hold values from 0 to 2
- zscores: bfloat16 [196608], P(('row', 'col')), may hold values from -18 to 18
- band_reach: int32 [256], replicated, may hold values from 0 to 2, as said below
Outputs:
- ld_tiles: bfloat16 [196608, 3840], P(('row', 'col'))
- smoothed: float32 [196608], P(('row', 'col'))
- quadratic: float32 [], replicated
Inputs may be any that keep to these rules, and one draw needn't show every extreme that they name: `band_reach`: the first 3 blocks, the last 3 blocks and some two neighbouring blocks reach 2.
All inputs are finite; a program needn't handle non-finite values.
Results may differ from a plain program's by a relative error of at most 0.0042.
Values may be sent and summed in bfloat16 or wider, within the bound.
A program may use at most 64 MiB of HBM per device.

v0:
```python
import jax
import jax.numpy as jnp
from jax import lax
from jax.sharding import Mesh
from jax.sharding import PartitionSpec as P

BAND = 2
ROW_COL = ("row_0", "row_1", "row_2", "col_0", "col_1")


def passed_along(value, axis, steps):
    count = lax.axis_size(axis)
    initial, last = (max(0, -steps), min(count, count - steps))
    return lax.ppermute(value, axis, [(source, source + steps) for source in range(initial, last)])


def by_axis(value, axes):
    for axis in axes:
        value = lax.psum(value, axis)
    return value


def standardize(dosage):
    values = dosage.astype(jnp.float32)
    column_mean = jnp.mean(values, axis=0)
    centered = values - column_mean
    variance = jnp.mean(centered * centered, axis=0)
    return (centered * lax.rsqrt(variance + 1e-05)).astype(jnp.bfloat16)


def body(dosage, zscores, band_reach):
    samples = dosage.shape[0]
    block_width = zscores.shape[0]
    block_count = lax.axis_size(ROW_COL)
    position = lax.axis_index(ROW_COL)
    scaled = standardize(dosage)
    own_reach = lax.dynamic_index_in_dim(band_reach, position, 0, False)

    def allowed(offset):
        other = position + offset
        inside = (other >= 0) & (other < block_count)
        their_reach = lax.dynamic_index_in_dim(
            band_reach, jnp.clip(other, 0, block_count - 1), 0, False
        )
        return inside & (abs(offset) <= jnp.minimum(own_reach, their_reach))

    def make_tile(left, right, offset):
        product = (
            lax.dot_general(
                left, right, (((0,), (0,)), ((), ())), preferred_element_type=jnp.float32
            )
            / samples
        )
        return jnp.where(allowed(offset), product, 0.0).astype(jnp.bfloat16)

    def apply_tile(ld_tile, near_scores):
        return jnp.dot(ld_tile, near_scores, preferred_element_type=jnp.float32)

    own_z = zscores.astype(jnp.float32)
    tile_map = {0: make_tile(scaled, scaled, 0)}
    score_map = {0: zscores}
    for offset in range(1, BAND + 1):
        far_scaled, far_z = passed_along((scaled, zscores), ROW_COL, -offset)
        tile_map[offset] = make_tile(scaled, far_scaled, offset)
        score_map[offset] = far_z
    terms = {}
    for offset in range(0, BAND + 1):
        terms[offset] = apply_tile(tile_map[offset], score_map[offset])
    total = None
    for offset in range(1, BAND + 1):
        returned, returned_z = passed_along((tile_map[offset], zscores), ROW_COL, offset)
        tile_map[-offset] = returned.T
        score_map[-offset] = returned_z
    for offset in range(1, BAND + 1):
        terms[-offset] = apply_tile(tile_map[-offset], score_map[-offset])
    smoothed = terms[0]
    for offset in range(1, BAND + 1):
        smoothed = smoothed + terms[offset] + terms[-offset]
    total = by_axis(jnp.sum(own_z * smoothed), ROW_COL)
    quadratic = total / (block_count * block_width)
    ld_tiles = jnp.concatenate([tile_map[offset] for offset in range(-BAND, BAND + 1)], axis=1)
    return (ld_tiles, smoothed, quadratic)


def solution(mesh):
    torus = Mesh(mesh.devices.reshape(4, 2, 2, 4, 4), ("row_0", "row_1", "row_2", "col_0", "col_1"))
    return jax.shard_map(
        body,
        mesh=torus,
        in_specs=(P(None, ROW_COL), P(ROW_COL), P()),
        out_specs=(P(ROW_COL, None), P(ROW_COL), P()),
        check_vma=False,
    )
```

profile of v0, /device:TPU:2, one launch (start us, length us, event | category | flops | bytes accessed | tf_op | source)
XLA Modules:
  0.0 394.4 jit_solution(10155190319292497556)
XLA Ops:
  0.6 0.0 copy-start
  0.6 2.2 convert_reduce_fusion
  2.9 0.1 copy-done
  3.0 0.7 fusion.2
  3.7 2.0 fusion.3
  5.7 9.6 %collective-permute-start.2 = (bf16[1536,768]{1,0:T(8,128)(2,1)}, bf16[1536,768]{1,0:T(8,128)(2,1)S(1)}, u32[]{:S(2)}, u32[]{:S(2)}) collective-permute-start(bf16[1536,768]{1,0:T(8,128)(2,1)} %fusion.3), channel_id=1, source_target_pairs={{1,0},{2,1},{3,2},{4,3},{5,4},{6,5},{7,6},{8,7},{9,8},{10,9},{11,1... | collective-permute-start | bytes 7077896 | tf_op jit(solution)/shard_map/ppermute | solution.py:14
  15.3 3.1 collective-permute-start
  18.4 0.6 fusion.10
  21.5 210.7 %collective-permute-done.2 = bf16[1536,768]{1,0:T(8,128)(2,1)S(1)} collective-permute-done((bf16[1536,768]{1,0:T(8,128)(2,1)}, bf16[1536,768]{1,0:T(8,128)(2,1)S(1)}, u32[]{:S(2)}, u32[]{:S(2)}) %collective-permute-start.2) | collective-permute-done | bytes 2359328 | tf_op jit(solution)/shard_map/ppermute | solution.py:14
  232.2 3.7 select_convert_fusion.1
  235.9 1.9 collective-permute-start.3
  237.8 46.4 %collective-permute-done = bf16[1536,768]{1,0:T(8,128)(2,1)} collective-permute-done((bf16[1536,768]{1,0:T(8,128)(2,1)}, bf16[1536,768]{1,0:T(8,128)(2,1)}, u32[]{:S(2)}, u32[]{:S(2)}) %collective-permute-start) | collective-permute-done | bytes 2359328 | tf_op jit(solution)/shard_map/ppermute | solution.py:14
  284.2 4.4 %select_convert_fusion.2 = bf16[768,768]{0,1:T(8,128)(2,1)S(1)} fusion(bf16[1536,768]{1,0:T(8,128)(2,1)} %fusion.3, bf16[1536,768]{1,0:T(8,128)(2,1)} %collective-permute-done, pred[]{:T(512)S(6)} %and.24), kind=kOutput, calls=%fused_computation.8 | convolution fusion | flops 1813708800 | bytes 5898241 | tf_op jit(solution)/shard_map/dot_general | solution.py:49
  288.6 0.0 copy-start.3
  288.6 1.4 copy.6
  290.1 1.9 collective-permute-start.1
  292.0 9.8 %collective-permute-start.6 = (bf16[768]{0:T(1024)(128)(2,1)S(1)}, bf16[768]{0:T(1024)(128)(2,1)S(1)}, u32[]{:S(2)}, u32[]{:S(2)}) collective-permute-start(bf16[768]{0:T(1024)(128)(2,1)S(1)} %copy-done.3), channel_id=1, source_target_pairs={{2,0},{3,1},{4,2},{5,3},{6,4},{7,5},{8,6},{9,7},{10,8},{11,9},{12,... | collective-permute-start | bytes 4616 | tf_op jit(solution)/shard_map/ppermute | solution.py:14
  301.9 1.9 collective-permute-start.5
  303.8 7.9 %collective-permute-start.4 = (bf16[768]{0:T(1024)(128)(2,1)S(1)}, bf16[768]{0:T(1024)(128)(2,1)}, u32[]{:S(2)}, u32[]{:S(2)}) collective-permute-start(bf16[768]{0:T(1024)(128)(2,1)S(1)} %copy-done.3), channel_id=1, source_target_pairs={{1,0},{2,1},{3,2},{4,3},{5,4},{6,5},{7,6},{8,7},{9,8},{10,9},{11,1... | collective-permute-start | bytes 4616 | tf_op jit(solution)/shard_map/ppermute | solution.py:14
  311.7 0.0 collective-permute-done.6
  311.7 1.9 collective-permute-start.7
  314.8 0.2 collective-permute-done.5
  315.0 0.0 collective-permute-done.4
  315.0 0.7 reshape.25
  315.7 7.0 %collective-permute-done.7 = bf16[768]{0:T(1024)(128)(2,1)} collective-permute-done((bf16[768]{0:T(1024)(128)(2,1)S(1)}, bf16[768]{0:T(1024)(128)(2,1)}, u32[]{:S(2)}, u32[]{:S(2)}) %collective-permute-start.7) | collective-permute-done | bytes 1568 | tf_op jit(solution)/shard_map/ppermute | solution.py:14
  322.7 1.2 reshape.31
  323.9 0.3 convolution_reduce_fusion.2
  324.2 0.3 convolution_reduce_fusion
  324.5 0.0 collective-permute-done.3
  324.5 1.5 copy.7
  326.0 0.0 collective-permute-done.1
  326.0 2.5 bitcast_dynamic-update-slice_fusion
  328.4 0.0 copy-done.1
  328.4 1.1 constant_dynamic-update-slice_fusion.3
  329.6 5.4 %constant_dynamic-update-slice_fusion.2 = (bf16[768,3840]{0,1:T(8,128)(2,1)}, bf16[768,768]{0,1:T(8,128)(2,1)S(1)}) fusion(bf16[768,3840]{0,1:T(8,128)(2,1)} %constant_dynamic-update-slice_fusion.3, bf16[1536,768]{1,0:T(8,128)(2,1)} %fusion.3, pred[]{:T(512)S(6)} %and.28), kind=kOutput, calls=%fused_computation.19 | convolution fusion | flops 1813708800 | bytes 7077889 | tf_op jit(solution)/shard_map/dot_general | solution.py:49
  335.0 0.3 convolution_reduce_fusion.3
  335.3 0.4 convolution_reduce_fusion.1
  335.8 0.0 copy-done.2
  335.8 1.6 fusion.6
  337.4 1.2 multiply_reduce_fusion
  338.6 8.5 %psum.35 = f32[]{:T(128)} all-reduce(f32[]{:T(128)} %get-tuple-element.6), channel_id=1, replica_groups=mesh['row_0'=4,'row_1'=2,'row_2'=2,'col_0'=4,'col_1'=4] {'row_0'}, use_global_device_ids=true, to_apply=%region_3.4 | all-reduce | flops 1 | bytes 8 | tf_op jit(solution)/shard_map/psum | solution.py:19
  347.0 5.5 %psum.36 = f32[]{:T(128)} all-reduce(f32[]{:T(128)} %psum.35), channel_id=1, replica_groups=mesh['row_0'=4,'row_1'=2,'row_2'=2,'col_0'=4,'col_1'=4] {'row_1'}, use_global_device_ids=true, to_apply=%region_4.5 | all-reduce | flops 1 | bytes 8 | tf_op jit(solution)/shard_map/psum | solution.py:19
  352.6 1.1 constant_dynamic-update-slice_fusion.1
  353.7 3.1 psum.37
  356.7 1.1 constant_dynamic-update-slice_fusion
  357.9 8.4 %psum.38 = f32[]{:T(128)} all-reduce(f32[]{:T(128)} %psum.37), channel_id=1, replica_groups=mesh['row_0'=4,'row_1'=2,'row_2'=2,'col_0'=4,'col_1'=4] {'col_0'}, use_global_device_ids=true, to_apply=%region_6.7 | all-reduce | flops 1 | bytes 8 | tf_op jit(solution)/shard_map/psum | solution.py:19
  366.3 8.4 %copy.8 = bf16[768,3840]{1,0:T(8,128)(2,1)} copy(bf16[768,3840]{0,1:T(8,128)(2,1)} %constant_dynamic-update-slice_fusion) | data formatting | bytes 11796480
  374.7 17.9 %psum.39 = f32[]{:T(128)} all-reduce(f32[]{:T(128)} %psum.38), channel_id=1, replica_groups=mesh['row_0'=4,'row_1'=2,'row_2'=2,'col_0'=4,'col_1'=4] {'col_1'}, use_global_device_ids=true, to_apply=%region_7.8 | all-reduce | flops 1 | bytes 8 | tf_op jit(solution)/shard_map/psum | solution.py:19
  (12 shorter events, 0.0 us)
Async XLA Ops:
  0.6 2.4 copy-start
  3.7 14.7 %copy-start.5 = (s32[256]{0:T(256)S(1)}, s32[256]{0:T(256)}, u32[]{:S(2)}) copy-start(s32[256]{0:T(256)} %param.5) | copy-start | bytes 3076
  5.7 226.5 %collective-permute-start.2 = (bf16[1536,768]{1,0:T(8,128)(2,1)}, bf16[1536,768]{1,0:T(8,128)(2,1)S(1)}, u32[]{:S(2)}, u32[]{:S(2)}) collective-permute-start(bf16[1536,768]{1,0:T(8,128)(2,1)} %fusion.3), channel_id=1, source_target_pairs={{1,0},{2,1},{3,2},{4,3},{5,4},{6,5},{7,6},{8,7},{9,8},{10,9},{11,1... | collective-permute-start | bytes 7077896 | tf_op jit(solution)/shard_map/ppermute | solution.py:14
  15.3 268.9 %collective-permute-start = (bf16[1536,768]{1,0:T(8,128)(2,1)}, bf16[1536,768]{1,0:T(8,128)(2,1)}, u32[]{:S(2)}, u32[]{:S(2)}) collective-permute-start(bf16[1536,768]{1,0:T(8,128)(2,1)} %fusion.3), channel_id=1, source_target_pairs={{2,0},{3,1},{4,2},{5,3},{6,4},{7,5},{8,6},{9,7},{10,8},{11,9},{12,... | collective-permute-start | bytes 7077896 | tf_op jit(solution)/shard_map/ppermute | solution.py:14
  235.9 88.6 %collective-permute-start.3 = (bf16[768,768]{0,1:T(8,128)(2,1)S(1)}, bf16[768,768]{0,1:T(8,128)(2,1)S(1)}, u32[]{:S(2)}, u32[]{:S(2)}) collective-permute-start(bf16[768,768]{0,1:T(8,128)(2,1)S(1)} %select_convert_fusion.1), channel_id=1, source_target_pairs={{0,1},{1,2},{2,3},{3,4},{4,5},{5,6},{6,7},{7,8},{8,9},{9,10},{10,1... | collective-permute-start | bytes 3538952 | tf_op jit(solution)/shard_map/ppermute | solution.py:14
  288.6 3.4 copy-start.3
  290.1 35.9 %collective-permute-start.1 = (bf16[768,768]{1,0:T(8,128)(2,1)}, bf16[768,768]{1,0:T(8,128)(2,1)}, u32[]{:S(2)}, u32[]{:S(2)}) collective-permute-start(bf16[768,768]{1,0:T(8,128)(2,1)} %copy.6), channel_id=1, source_target_pairs={{0,2},{1,3},{2,4},{3,5},{4,6},{5,7},{6,8},{7,9},{8,10},{9,11},{10,... | collective-permute-start | bytes 3538952 | tf_op jit(solution)/shard_map/ppermute | solution.py:14
  292.0 19.6 %collective-permute-start.6 = (bf16[768]{0:T(1024)(128)(2,1)S(1)}, bf16[768]{0:T(1024)(128)(2,1)S(1)}, u32[]{:S(2)}, u32[]{:S(2)}) collective-permute-start(bf16[768]{0:T(1024)(128)(2,1)S(1)} %copy-done.3), channel_id=1, source_target_pairs={{2,0},{3,1},{4,2},{5,3},{6,4},{7,5},{8,6},{9,7},{10,8},{11,9},{12,... | collective-permute-start | bytes 4616 | tf_op jit(solution)/shard_map/ppermute | solution.py:14
  301.9 13.2 %collective-permute-start.5 = (bf16[768]{0:T(1024)(128)(2,1)S(1)}, bf16[768]{0:T(1024)(128)(2,1)S(1)}, u32[]{:S(2)}, u32[]{:S(2)}) collective-permute-start(bf16[768]{0:T(1024)(128)(2,1)S(1)} %copy-done.3), channel_id=1, source_target_pairs={{0,1},{1,2},{2,3},{3,4},{4,5},{5,6},{6,7},{7,8},{8,9},{9,10},{10,1... | collective-permute-start | bytes 4616 | tf_op jit(solution)/shard_map/ppermute | solution.py:14
  303.8 11.2 %collective-permute-start.4 = (bf16[768]{0:T(1024)(128)(2,1)S(1)}, bf16[768]{0:T(1024)(128)(2,1)}, u32[]{:S(2)}, u32[]{:S(2)}) collective-permute-start(bf16[768]{0:T(1024)(128)(2,1)S(1)} %copy-done.3), channel_id=1, source_target_pairs={{1,0},{2,1},{3,2},{4,3},{5,4},{6,5},{7,6},{8,7},{9,8},{10,9},{11,1... | collective-permute-start | bytes 4616 | tf_op jit(solution)/shard_map/ppermute | solution.py:14
  311.7 11.0 %collective-permute-start.7 = (bf16[768]{0:T(1024)(128)(2,1)S(1)}, bf16[768]{0:T(1024)(128)(2,1)}, u32[]{:S(2)}, u32[]{:S(2)}) collective-permute-start(bf16[768]{0:T(1024)(128)(2,1)S(1)} %copy-done.3), channel_id=1, source_target_pairs={{0,2},{1,3},{2,4},{3,5},{4,6},{5,7},{6,8},{7,9},{8,10},{9,11},{10,... | collective-permute-start | bytes 4616 | tf_op jit(solution)/shard_map/ppermute | solution.py:14
  326.0 2.5 copy-start.1
  335.0 0.8 copy-start.2
  335.0 2.3 copy-start.4
where the time goes:
time: 395 us; the launch traced here: 394 us
  waiting for transfers between devices  264 us (67%)
  blocking collectives  43.4 us (11%)
  starting transfers between devices  38.1 us (10%)
  local copies, waits for them, and re-layouts  19.8 us (5%)
  matrix products  16.4 us (4%)
  between operations  6.27 us (2%)
  other arithmetic  6.11 us (2%)
    ppermute x8, waiting for transfers between devices, passed_along(): lax.ppermute(value, axis, [(source, source + steps) for source in range(i...  264 us
    psum x5, blocking collectives, by_axis(): value = lax.psum(value, axis)  43.4 us
    ppermute x8, starting transfers between devices, passed_along(): lax.ppermute(value, axis, [(source, source + steps) for source in range(i...  38.1 us
    dot_general x3, matrix products, make_tile(): lax.dot_general(left, right, (((0,), (0,)), ((), ())), preferred_element_...  13.6 us
    unnamed x17, local copies, waits for them, and re-layouts  13.2 us
  transfers between devices with their start and end apart: 8, of which 4 were waited for; matrix products, arithmetic and copies ran while one was open for 4% of the time, Pallas kernels for 0%

commit v1 on v0

--- a/solution.py
+++ b/solution.py
@@ -8,6 +8,12 @@
 ROW_COL = ("row_0", "row_1", "row_2", "col_0", "col_1")
 
 
+def gather_and_add(shard, mesh_axis):
+    pieces = lax.all_gather(shard, mesh_axis, axis=0, tiled=False)
+    result = pieces.sum(axis=0)
+    return result
+
+
 def passed_along(value, axis, steps):
     count = lax.axis_size(axis)
     initial, last = (max(0, -steps), min(count, count - steps))
@@ -16,7 +22,7 @@
 
 def by_axis(value, axes):
     for axis in axes:
-        value = lax.psum(value, axis)
+        value = gather_and_add(value, axis)
     return value
 
 

time: 395 us -> 405 us (1.025)
  local copies, waits for them, and re-layouts: 19.8 us -> 33.2 us
    psum x5 -> x0, blocking collectives: 43.4 us -> none  [by_axis(): value = lax.psum(value, axis)]
    unnamed x0 -> x5, blocking collectives: none -> 40.8 us
    unnamed x17 -> x32, local copies, waits for them, and re-layouts: 13.2 us -> 26.6 us
    ppermute x8, waiting for transfers between devices: 264 us -> 260 us  [passed_along(): lax.ppermute(value, axis, [(source, source + steps) for source in range(i...]
  transfers between devices with their start and end apart: 8 -> 8, of which waited for: 4 -> 3; matrix products, arithmetic and copies ran while one was open for 4% -> 5% of each run, Pallas kernels for 0% -> 0%
where the time goes in v1:
time: 405 us; the launch traced here: 404 us
  waiting for transfers between devices  260 us (64%)
  blocking collectives  40.8 us (10%)
  starting transfers between devices  38.1 us (9%)
  local copies, waits for them, and re-layouts  33.2 us (8%)
  matrix products  17.1 us (4%)
  other arithmetic  9.13 us (2%)
  between operations  6.29 us (2%)
    ppermute x8, waiting for transfers between devices, passed_along(): lax.ppermute(value, axis, [(source, source + steps) for source in range(i...  260 us
    unnamed x5, blocking collectives  40.8 us
    ppermute x8, starting transfers between devices, passed_along(): lax.ppermute(value, axis, [(source, source + steps) for source in range(i...  38.1 us
    unnamed x32, local copies, waits for them, and re-layouts  26.6 us
    dot_general x3, matrix products, make_tile(): lax.dot_general(left, right, (((0,), (0,)), ((), ())), preferred_element_...  14.3 us
  transfers between devices with their start and end apart: 8, of which 3 were waited for; matrix products, arithmetic and copies ran while one was open for 5% of the time, Pallas kernels for 0%

profile of v1, /device:TPU:2, one launch (start us, length us, event | category | flops | bytes accessed | tf_op | source)
XLA Modules:
  0.0 404.3 jit_solution(126198414085689906)
XLA Ops:
  0.6 2.2 convert_reduce_fusion
  3.0 0.7 fusion.2
  3.7 2.0 fusion.3
  5.7 9.6 %collective-permute-start.2 = (bf16[1536,768]{1,0:T(8,128)(2,1)}, bf16[1536,768]{1,0:T(8,128)(2,1)}, u32[]{:S(2)}, u32[]{:S(2)}) collective-permute-start(bf16[1536,768]{1,0:T(8,128)(2,1)} %fusion.3), channel_id=1, source_target_pairs={{1,0},{2,1},{3,2},{4,3},{5,4},{6,5},{7,6},{8,7},{9,8},{10,9},{11,1... | collective-permute-start | bytes 7077896 | tf_op jit(solution)/shard_map/ppermute | solution.py:20
  15.3 3.1 collective-permute-start
  18.4 0.7 fusion.10
  21.5 210.7 %collective-permute-done.2 = bf16[1536,768]{1,0:T(8,128)(2,1)} collective-permute-done((bf16[1536,768]{1,0:T(8,128)(2,1)}, bf16[1536,768]{1,0:T(8,128)(2,1)}, u32[]{:S(2)}, u32[]{:S(2)}) %collective-permute-start.2) | collective-permute-done | bytes 2359328 | tf_op jit(solution)/shard_map/ppermute | solution.py:20
  232.2 4.4 %select_convert_fusion.1 = bf16[768,768]{0,1:T(8,128)(2,1)S(1)} fusion(bf16[1536,768]{1,0:T(8,128)(2,1)} %fusion.3, bf16[1536,768]{1,0:T(8,128)(2,1)} %collective-permute-done.2, pred[]{:T(512)S(6)} %and.26), kind=kOutput, calls=%fused_computation.7 | convolution fusion | flops 1813708800 | bytes 5898241 | tf_op jit(solution)/shard_map/dot_general | solution.py:55
  236.6 1.9 collective-permute-start.3
  238.5 45.7 %collective-permute-done = bf16[1536,768]{1,0:T(8,128)(2,1)} collective-permute-done((bf16[1536,768]{1,0:T(8,128)(2,1)}, bf16[1536,768]{1,0:T(8,128)(2,1)}, u32[]{:S(2)}, u32[]{:S(2)}) %collective-permute-start) | collective-permute-done | bytes 2359328 | tf_op jit(solution)/shard_map/ppermute | solution.py:20
  284.2 4.4 %select_convert_fusion.2 = bf16[768,768]{0,1:T(8,128)(2,1)S(1)} fusion(bf16[1536,768]{1,0:T(8,128)(2,1)} %fusion.3, bf16[1536,768]{1,0:T(8,128)(2,1)} %collective-permute-done, pred[]{:T(512)S(6)} %and.24), kind=kOutput, calls=%fused_computation.8 | convolution fusion | flops 1813708800 | bytes 5898241 | tf_op jit(solution)/shard_map/dot_general | solution.py:55
  288.7 1.4 copy.6
  290.1 1.9 collective-permute-start.1
  292.0 9.8 %collective-permute-start.6 = (bf16[768]{0:T(1024)(128)(2,1)S(1)}, bf16[768]{0:T(1024)(128)(2,1)S(1)}, u32[]{:S(2)}, u32[]{:S(2)}) collective-permute-start(bf16[768]{0:T(1024)(128)(2,1)S(1)} %copy-done.3), channel_id=1, source_target_pairs={{2,0},{3,1},{4,2},{5,3},{6,4},{7,5},{8,6},{9,7},{10,8},{11,9},{12,... | collective-permute-start | bytes 4616 | tf_op jit(solution)/shard_map/ppermute | solution.py:20
  301.9 1.9 collective-permute-start.5
  303.8 7.9 %collective-permute-start.4 = (bf16[768]{0:T(1024)(128)(2,1)S(1)}, bf16[768]{0:T(1024)(128)(2,1)}, u32[]{:S(2)}, u32[]{:S(2)}) collective-permute-start(bf16[768]{0:T(1024)(128)(2,1)S(1)} %copy-done.3), channel_id=1, source_target_pairs={{1,0},{2,1},{3,2},{4,3},{5,4},{6,5},{7,6},{8,7},{9,8},{10,9},{11,1... | collective-permute-start | bytes 4616 | tf_op jit(solution)/shard_map/ppermute | solution.py:20
  311.7 1.9 collective-permute-start.7
  313.6 1.3 dynamic-slice.4
  314.9 1.3 dynamic-slice.3
  316.2 1.3 dynamic-slice
  318.8 0.7 reshape.50
  319.5 3.2 collective-permute-done.7
  322.7 1.2 reshape.56
  324.5 1.5 copy.7
  326.0 2.5 bitcast_dynamic-update-slice_fusion
  328.4 1.1 constant_dynamic-update-slice_fusion.3
  329.6 5.4 %constant_dynamic-update-slice_fusion.2 = (bf16[768,3840]{0,1:T(8,128)(2,1)}, bf16[768,768]{0,1:T(8,128)(2,1)S(1)}) fusion(bf16[768,3840]{0,1:T(8,128)(2,1)} %constant_dynamic-update-slice_fusion.3, bf16[1536,768]{1,0:T(8,128)(2,1)} %fusion.3, pred[]{:T(512)S(6)} %and.28), kind=kOutput, calls=%fused_computation.19 | convolution fusion | flops 1813708800 | bytes 7077889 | tf_op jit(solution)/shard_map/dot_general | solution.py:55
  335.8 1.6 fusion.6
  337.4 1.2 multiply_reduce_fusion
  338.6 1.4 dynamic-update-slice
  339.9 1.3 dynamic-slice.1
  341.2 8.5 %all-reduce = f32[4]{0:T(128)S(1)} all-reduce(f32[4]{0:T(128)S(1)} %dynamic-update-slice), channel_id=1, replica_groups=mesh['row_0'=4,'row_1'=2,'row_2'=2,'col_0'=4,'col_1'=4] {'row_0'}, use_global_device_ids=true, to_apply=%add | all-reduce | flops 4 | bytes 32
  349.7 0.6 reduce_sum.75
  350.3 1.4 dynamic-update-slice.1
  351.7 1.3 dynamic-slice.2
  353.0 4.9 %all-reduce.1 = f32[2]{0:T(128)S(1)} all-reduce(f32[2]{0:T(128)S(1)} %dynamic-update-slice.1), channel_id=1, replica_groups=mesh['row_0'=4,'row_1'=2,'row_2'=2,'col_0'=4,'col_1'=4] {'row_1'}, use_global_device_ids=true, to_apply=%add.1 | all-reduce | flops 2 | bytes 16
  357.9 0.6 reduce_sum.76
  358.5 1.4 dynamic-update-slice.2
  359.9 1.1 constant_dynamic-update-slice_fusion.1
  361.0 2.4 all-reduce.2
  363.4 0.6 reduce_sum.77
  364.0 1.4 dynamic-update-slice.3
  365.5 1.1 constant_dynamic-update-slice_fusion
  366.6 12.5 %all-reduce.3 = f32[4]{0:T(128)S(1)} all-reduce(f32[4]{0:T(128)S(1)} %dynamic-update-slice.3), channel_id=1, replica_groups=mesh['row_0'=4,'row_1'=2,'row_2'=2,'col_0'=4,'col_1'=4] {'col_0'}, use_global_device_ids=true, to_apply=%add.3 | all-reduce | flops 4 | bytes 32
  379.1 0.6 reduce_sum.78
  379.7 1.3 dynamic-update-slice.4
  381.0 8.4 %copy.8 = bf16[768,3840]{1,0:T(8,128)(2,1)} copy(bf16[768,3840]{0,1:T(8,128)(2,1)} %constant_dynamic-update-slice_fusion) | data formatting | bytes 11796480
  389.4 12.5 %all-reduce.4 = f32[4]{0:T(128)S(1)} all-reduce(f32[4]{0:T(128)S(1)} %dynamic-update-slice.4), channel_id=1, replica_groups=mesh['row_0'=4,'row_1'=2,'row_2'=2,'col_0'=4,'col_1'=4] {'col_1'}, use_global_device_ids=true, to_apply=%add.4 | all-reduce | flops 4 | bytes 32
  (32 shorter events, 2.1 us)
Async XLA Ops:
  0.6 2.4 copy-start
  3.7 14.7 %copy-start.5 = (s32[256]{0:T(256)S(1)}, s32[256]{0:T(256)}, u32[]{:S(2)}) copy-start(s32[256]{0:T(256)} %param.5) | copy-start | bytes 3076
  5.7 226.5 %collective-permute-start.2 = (bf16[1536,768]{1,0:T(8,128)(2,1)}, bf16[1536,768]{1,0:T(8,128)(2,1)}, u32[]{:S(2)}, u32[]{:S(2)}) collective-permute-start(bf16[1536,768]{1,0:T(8,128)(2,1)} %fusion.3), channel_id=1, source_target_pairs={{1,0},{2,1},{3,2},{4,3},{5,4},{6,5},{7,6},{8,7},{9,8},{10,9},{11,1... | collective-permute-start | bytes 7077896 | tf_op jit(solution)/shard_map/ppermute | solution.py:20
  15.3 268.9 %collective-permute-start = (bf16[1536,768]{1,0:T(8,128)(2,1)}, bf16[1536,768]{1,0:T(8,128)(2,1)}, u32[]{:S(2)}, u32[]{:S(2)}) collective-permute-start(bf16[1536,768]{1,0:T(8,128)(2,1)} %fusion.3), channel_id=1, source_target_pairs={{2,0},{3,1},{4,2},{5,3},{6,4},{7,5},{8,6},{9,7},{10,8},{11,9},{12,... | collective-permute-start | bytes 7077896 | tf_op jit(solution)/shard_map/ppermute | solution.py:20
  236.6 87.9 %collective-permute-start.3 = (bf16[768,768]{0,1:T(8,128)(2,1)S(1)}, bf16[768,768]{0,1:T(8,128)(2,1)S(1)}, u32[]{:S(2)}, u32[]{:S(2)}) collective-permute-start(bf16[768,768]{0,1:T(8,128)(2,1)S(1)} %select_convert_fusion.1), channel_id=1, source_target_pairs={{0,1},{1,2},{2,3},{3,4},{4,5},{5,6},{6,7},{7,8},{8,9},{9,10},{10,1... | collective-permute-start | bytes 3538952 | tf_op jit(solution)/shard_map/ppermute | solution.py:20
  288.6 3.4 copy-start.3
  290.1 35.9 %collective-permute-start.1 = (bf16[768,768]{1,0:T(8,128)(2,1)}, bf16[768,768]{1,0:T(8,128)(2,1)}, u32[]{:S(2)}, u32[]{:S(2)}) collective-permute-start(bf16[768,768]{1,0:T(8,128)(2,1)} %copy.6), channel_id=1, source_target_pairs={{0,2},{1,3},{2,4},{3,5},{4,6},{5,7},{6,8},{7,9},{8,10},{9,11},{10,... | collective-permute-start | bytes 3538952 | tf_op jit(solution)/shard_map/ppermute | solution.py:20
  292.0 19.6 %collective-permute-start.6 = (bf16[768]{0:T(1024)(128)(2,1)S(1)}, bf16[768]{0:T(1024)(128)(2,1)S(1)}, u32[]{:S(2)}, u32[]{:S(2)}) collective-permute-start(bf16[768]{0:T(1024)(128)(2,1)S(1)} %copy-done.3), channel_id=1, source_target_pairs={{2,0},{3,1},{4,2},{5,3},{6,4},{7,5},{8,6},{9,7},{10,8},{11,9},{12,... | collective-permute-start | bytes 4616 | tf_op jit(solution)/shard_map/ppermute | solution.py:20
  301.9 16.9 %collective-permute-start.5 = (bf16[768]{0:T(1024)(128)(2,1)S(1)}, bf16[768]{0:T(1024)(128)(2,1)S(1)}, u32[]{:S(2)}, u32[]{:S(2)}) collective-permute-start(bf16[768]{0:T(1024)(128)(2,1)S(1)} %copy-done.3), channel_id=1, source_target_pairs={{0,1},{1,2},{2,3},{3,4},{4,5},{5,6},{6,7},{7,8},{8,9},{9,10},{10,1... | collective-permute-start | bytes 4616 | tf_op jit(solution)/shard_map/ppermute | solution.py:20
  303.8 15.0 %collective-permute-start.4 = (bf16[768]{0:T(1024)(128)(2,1)S(1)}, bf16[768]{0:T(1024)(128)(2,1)}, u32[]{:S(2)}, u32[]{:S(2)}) collective-permute-start(bf16[768]{0:T(1024)(128)(2,1)S(1)} %copy-done.3), channel_id=1, source_target_pairs={{1,0},{2,1},{3,2},{4,3},{5,4},{6,5},{7,6},{8,7},{9,8},{10,9},{11,1... | collective-permute-start | bytes 4616 | tf_op jit(solution)/shard_map/ppermute | solution.py:20
  311.7 11.0 %collective-permute-start.7 = (bf16[768]{0:T(1024)(128)(2,1)S(1)}, bf16[768]{0:T(1024)(128)(2,1)}, u32[]{:S(2)}, u32[]{:S(2)}) collective-permute-start(bf16[768]{0:T(1024)(128)(2,1)S(1)} %copy-done.3), channel_id=1, source_target_pairs={{0,2},{1,3},{2,4},{3,5},{4,6},{5,7},{6,8},{7,9},{8,10},{9,11},{10,... | collective-permute-start | bytes 4616 | tf_op jit(solution)/shard_map/ppermute | solution.py:20
  326.0 2.5 copy-start.1
  335.0 0.8 copy-start.2
  335.0 2.3 copy-start.4
